TPU v7x, 32 devices: a whole 2x2x4 slice. The times are simulated.
32 devices in a mesh: chan: 4 (over z), tm: 8 (over y, x, core).
Axes of the slice: x: 2, y: 2, z: 4, core: 2. Of those that a mesh axis runs over, the one named last changes fastest.
Arguments:
- trajectory: float32 [512, 8, 4096], P('tm', None, 'chan'), may hold values from -40 to 40
- initial: float32 [8, 4096], P(None, 'chan'), may hold values from -6 to 6
- drive_gate: bfloat16 [512, 8, 4096], P('tm', None, 'chan'), may hold values from -16 to 4
- drive_candidate: bfloat16 [512, 8, 4096], P('tm', None, 'chan'), may hold values from -6 to 6
- gate_weight: bfloat16 [4096, 4096], P('chan'), may hold values from -0.0234375 to 0.0234375
- candidate_weight: bfloat16 [4096, 4096], P('chan'), may hold values from -0.09375 to 0.09375
Outputs:
- newton_states: float32 [512, 8, 4096], P('tm', None, 'chan')
- residual_norm: float32 [], replicated
All inputs are finite; a program needn't handle non-finite values.
Results may differ from a plain program's by a relative error of at most 0.0016.
Values may be sent and summed in bfloat16 or wider, within the bound.
A program may use at most 128 MiB of HBM per device.

v0:
```python
import functools

import jax
import jax.numpy as jnp
from jax import lax
from jax.experimental import pallas as pl
from jax.experimental.pallas import tpu as pltpu
from jax.sharding import PartitionSpec as P

MESH = pl.DeviceIdType.MESH
BF16 = jnp.bfloat16
F32 = jnp.float32


def kernel(
    nz, nt, chunks, tile,
    traj, init, drive_g, drive_c, gate_w, cand_w,
    out, total,
    wbuf, abuf, prev0, diag, prod, carry, ssq, partner_map, maps, tsums, zsums,
    local_sem, wz_send, wz_recv, wx_send, wx_recv, wc_send, wc_recv,
    a_send, a_recv, row_sem, pm_sem, m_send, m_recv, ts_send, ts_recv, zs_send, zs_recv,
):
    z = lax.axis_index("chan")
    t = lax.axis_index("tm")
    steps, batch, width = traj.shape
    nc = nt // 2
    chip = lax.div(t, 2)
    core = lax.rem(t, 2)
    partner = (z, t + 1 - 2 * core)
    part = width // nt
    weights = (gate_w, cand_w)
    rows = steps * batch // chunks
    chunk_steps = steps // chunks

    def remote(src, dst, send, recv, device):
        return pltpu.make_async_remote_copy(
            src_ref=src, dst_ref=dst, send_sem=send, recv_sem=recv,
            device_id=device, device_id_type=MESH,
        )

    def zmod(v):
        return lax.rem(v + 2 * nz, nz)

    def cmod(v):
        return lax.rem(v + 2 * nc, nc)

    def wslot(g, source, p):
        return wbuf.at[g, pl.ds(pl.multiple_of(source * width + p * part, 16), part), :]

    barrier = pltpu.get_barrier_semaphore()
    for d in range(1, nz):
        pl.semaphore_signal(barrier, inc=1, device_id=(zmod(z + d), t), device_id_type=MESH)
    for d in range(1, nt):
        pl.semaphore_signal(barrier, inc=1, device_id=(z, lax.rem(t + d, nt)), device_id_type=MESH)
    pl.semaphore_wait(barrier, nz - 1 + nt - 1)

    sent = []

    def row_copy():
        return remote(traj.at[steps - 1], prev0, row_sem.at[0], row_sem.at[1], (z, lax.rem(t + 1, nt)))

    row_copy().start()

    def z_copy(d, g):
        other = zmod(z + d)
        src = weights[g].at[
            pl.ds(pl.multiple_of(t * part, 16), part), pl.ds(pl.multiple_of(other * width, 128), width)
        ]
        return remote(src, wslot(g, z, t), wz_send.at[g, d - 1], wz_recv.at[g, d - 1], (other, t))

    for d in range(1, nz):
        for g in range(2):
            z_copy(d, g).start()

    def own_copy(g):
        return pltpu.make_async_copy(
            weights[g].at[:, pl.ds(pl.multiple_of(z * width, 128), width)],
            wbuf.at[g, pl.ds(pl.multiple_of(z * width, 128), width), :],
            local_sem.at[g],
        )

    for g in range(2):
        own_copy(g).start()

    own_columns = pl.ds(pl.multiple_of(z * width, 128), width)

    @pl.loop(1, steps // 2)
    def _(j):
        pair = traj[pl.ds(2 * j - 1, 2)].reshape(2 * batch, width)
        abuf[pl.ds(pl.multiple_of(j * 2 * batch, 16), 2 * batch), own_columns] = pair.astype(BF16)

    row_copy().wait()

    @pl.when(t == 0)
    def _():
        prev0[...] = init[...]

    first = jnp.concatenate([prev0[...], traj[0]], 0)
    abuf[pl.ds(0, 2 * batch), own_columns] = first.astype(BF16)

    def a_copy(direction, source, i):
        slot = abuf.at[pl.ds(i * rows, rows), pl.ds(pl.multiple_of(source * width, 128), width)]
        to = z + 1 if direction == 0 else z - 1
        return remote(slot, slot, a_send.at[direction, source, i], a_recv.at[source, i], (to, t))

    for i in range(chunks):
        @pl.when(z < nz - 1)
        def _():
            a_copy(0, z, i).start()

        @pl.when(z > 0)
        def _():
            a_copy(1, z, i).start()

    for g in range(2):
        own_copy(g).wait()
        for j in range(width // 128):
            block = wbuf[g, pl.ds(pl.multiple_of(z * width + j * 128, 128), 128), pl.ds(j * 128, 128)]
            eye = lax.broadcasted_iota(jnp.int32, (128, 128), 0) == lax.broadcasted_iota(
                jnp.int32, (128, 128), 1
            )
            line = jnp.sum(jnp.where(eye, block.astype(F32), 0.0), axis=0, keepdims=True)
            diag[g, :, pl.ds(j * 128, 128)] = jnp.broadcast_to(line, (batch, 128))

    carry[0] = jnp.ones((batch, width), F32)
    carry[1] = jnp.zeros((batch, width), F32)
    ssq[...] = jnp.zeros((batch, width), F32)

    def x_copy(d, g, dq):
        slot = wslot(g, zmod(z - d), t)
        return remote(
            slot, slot, wx_send.at[g, d - 1, dq - 1], wx_recv.at[g, d - 1, dq - 1],
            (z, 2 * cmod(chip + dq) + core),
        )

    def c_copy(d, g, dq, side):
        slot = wslot(g, zmod(z - d), 2 * cmod(chip - dq) + side)
        return remote(slot, slot, wc_send.at[g, d - 1, dq], wc_recv.at[g, d - 1, dq], partner)

    def x_arrival(d, g, dq):
        slot = wslot(g, zmod(z - d), 2 * cmod(chip - dq) + core)
        return remote(slot, slot, wx_send.at[g, d - 1, dq - 1], wx_recv.at[g, d - 1, dq - 1], partner)

    def z_arrival(d, g):
        slot = wslot(g, zmod(z - d), t)
        return remote(slot, slot, wz_send.at[g, d - 1], wz_recv.at[g, d - 1], partner)

    for d in range(1, nz):
        for g in range(2):
            z_arrival(d, g).wait_recv()
            for dq in range(1, nc):
                x_copy(d, g, dq).start()
            c_copy(d, g, 0, core).start()

    onward = [(d, g, dq) for d in range(1, nz) for g in range(2) for dq in range(1, nc)]

    def relay(d, i):
        @pl.when(z - d >= 0)
        def _():
            a_copy(0, z - d, i).wait_recv()

            @pl.when(z < nz - 1)
            def _():
                a_copy(0, z - d, i).start()

        @pl.when(z + d < nz)
        def _():
            a_copy(1, z + d, i).wait_recv()

            @pl.when(z > 0)
            def _():
                a_copy(1, z + d, i).start()

    early = [(d, i) for d in range(1, nz - 1) for i in range(chunks)]
    spread = max(1, (3 * len(early)) // 4)
    per = -(-len(onward) // spread)
    for n, (d, i) in enumerate(early):
        relay(d, i)
        for item in onward[n * per : (n + 1) * per]:
            x_arrival(*item).wait_recv()
            c_copy(*item, core).start()
    for d in range(1, nz):
        for g in range(2):
            for dq in range(nc):
                c_copy(d, g, dq, 1 - core).wait_recv()

    def compute(i):
        @pl.loop(0, width // tile)
        def _(n):
            cols = pl.ds(pl.multiple_of(n * tile, tile), tile)
            lhs = abuf[pl.ds(i * rows, rows), :]
            shape = (chunk_steps, batch, tile)
            span = pl.ds(i * chunk_steps, chunk_steps)
            gate_pre = jnp.dot(lhs, wbuf[0, :, cols], preferred_element_type=F32).reshape(shape)
            cand_pre = jnp.dot(lhs, wbuf[1, :, cols], preferred_element_type=F32).reshape(shape)
            gate_pre = gate_pre + drive_g[span, :, cols].astype(F32)
            cand_pre = cand_pre + drive_c[span, :, cols].astype(F32)
            guess = traj[span, :, cols]
            if i == 0:
                previous = jnp.concatenate([prev0[:, cols][None], guess[:-1]], 0)
            else:
                previous = traj[pl.ds(i * chunk_steps - 1, chunk_steps), :, cols]
            update = jax.nn.sigmoid(gate_pre)
            candidate = jnp.tanh(cand_pre)
            keep = 1.0 - update
            mapped = keep * previous + update * candidate
            jacobian = (
                keep
                + update * keep * (candidate - previous) * diag[0, :, cols][None]
                + update * (1.0 - candidate * candidate) * diag[1, :, cols][None]
            )
            offset = mapped - jacobian * previous
            missing = guess - mapped
            ssq[:, cols] += jnp.sum(missing * missing, axis=0)
            product = carry[0, :, cols]
            state = carry[1, :, cols]
            for s in range(chunk_steps):
                product = jacobian[s] * product
                state = jacobian[s] * state + offset[s]
                prod[i * chunk_steps + s, :, cols] = product
                out[i * chunk_steps + s, :, cols] = state
            carry[0, :, cols] = product
            carry[1, :, cols] = state

    for i in range(chunks):
        relay(nz - 1, i)
        compute(i)

    def pm_copy():
        return remote(carry, partner_map, pm_sem.at[0], pm_sem.at[1], partner)

    pm_copy().start()
    mine = ssq[:, pl.ds(0, 128)]
    for j in range(1, width // 128):
        mine = mine + ssq[:, pl.ds(j * 128, 128)]
    tsums[t] = mine

    def ts_copy(d):
        slot = tsums.at[t]
        return remote(slot, slot, ts_send.at[d - 1], ts_recv.at[d - 1], (z, lax.rem(t + d, nt)))

    def ts_arrival(d):
        slot = tsums.at[lax.rem(t + nt - d, nt)]
        return remote(slot, slot, ts_send.at[d - 1], ts_recv.at[d - 1], partner)

    for d in range(1, nt):
        ts_copy(d).start()

    def m_copy(dq):
        slot = maps.at[chip]
        return remote(
            slot, slot, m_send.at[dq - 1], m_recv.at[dq - 1], (z, 2 * cmod(chip + dq) + core)
        )

    def m_arrival(dq):
        slot = maps.at[cmod(chip - dq)]
        return remote(slot, slot, m_send.at[dq - 1], m_recv.at[dq - 1], partner)

    pm_copy().wait()
    is_second = core == 1
    p_mine, s_mine, p_other, s_other = carry[0], carry[1], partner_map[0], partner_map[1]
    p_late = jnp.where(is_second, p_mine, p_other)
    s_early = jnp.where(is_second, s_other, s_mine)
    s_late = jnp.where(is_second, s_mine, s_other)
    maps[chip, 0] = p_mine * p_other
    maps[chip, 1] = p_late * s_early + s_late
    for dq in range(1, nc):
        m_copy(dq).start()

    for d in range(1, nt):
        ts_arrival(d).wait_recv()
    plane = tsums[0]
    for k in range(1, nt):
        plane = plane + tsums[k]
    zsums[z] = plane

    def zs_copy(d):
        slot = zsums.at[z]
        return remote(slot, slot, zs_send.at[d - 1], zs_recv.at[d - 1], (zmod(z + d), t))

    def zs_arrival(d):
        slot = zsums.at[zmod(z - d)]
        return remote(slot, slot, zs_send.at[d - 1], zs_recv.at[d - 1], partner)

    for d in range(1, nz):
        zs_copy(d).start()

    for dq in range(1, nc):
        m_arrival(dq).wait_recv()
    entry = init[...]
    for q in range(nc):
        entry = jnp.where(q < chip, maps[q, 0] * entry + maps[q, 1], entry)
    entry = jnp.where(is_second, p_other * entry + s_other, entry)
    carry_entry = entry
    prev0[...] = carry_entry

    @pl.loop(0, steps)
    def _(s):
        out[s] = prod[s] * prev0[...] + out[s]

    for d in range(1, nz):
        zs_arrival(d).wait_recv()
    whole = zsums[0]
    for k in range(1, nz):
        whole = whole + zsums[k]
    total[...] = whole

    for d in range(1, nz):
        zs_copy(d).wait_send()
        for g in range(2):
            z_copy(d, g).wait_send()
            for dq in range(1, nc):
                x_copy(d, g, dq).wait_send()
            for dq in range(nc):
                c_copy(d, g, dq, core).wait_send()
    for d in range(1, nt):
        ts_copy(d).wait_send()
    for dq in range(1, nc):
        m_copy(dq).wait_send()
    for i in range(chunks):
        for source in range(nz):
            @pl.when(jnp.logical_and(source <= z, z < nz - 1))
            def _():
                a_copy(0, source, i).wait_send()

            @pl.when(jnp.logical_and(source >= z, z > 0))
            def _():
                a_copy(1, source, i).wait_send()


def local(nz, nt, trajectory, initial, drive_gate, drive_candidate, gate_weight, candidate_weight):
    steps, batch, width = trajectory.shape
    nc = nt // 2
    full = gate_weight.shape[1]
    chunks = 4
    tile = min(256, width)
    dma = pltpu.SemaphoreType.DMA
    vmem = pl.BlockSpec(memory_space=pltpu.VMEM)
    hbm = pl.BlockSpec(memory_space=pl.ANY)
    states, total = pl.pallas_call(
        functools.partial(kernel, nz, nt, chunks, tile),
        out_shape=(
            jax.ShapeDtypeStruct((steps, batch, width), F32),
            jax.ShapeDtypeStruct((batch, 128), F32),
        ),
        in_specs=[vmem, vmem, vmem, vmem, hbm, hbm],
        out_specs=(vmem, vmem),
        scratch_shapes=[
            pltpu.VMEM((2, full, width), BF16),
            pltpu.VMEM((steps * batch, full), BF16),
            pltpu.VMEM((batch, width), F32),
            pltpu.VMEM((2, batch, width), F32),
            pltpu.VMEM((steps, batch, width), F32),
            pltpu.VMEM((2, batch, width), F32),
            pltpu.VMEM((batch, width), F32),
            pltpu.VMEM((2, batch, width), F32),
            pltpu.VMEM((nc, 2, batch, width), F32),
            pltpu.VMEM((nt, batch, 128), F32),
            pltpu.VMEM((nz, batch, 128), F32),
            dma((2,)),
            dma((2, nz - 1)),
            dma((2, nz - 1)),
            dma((2, nz - 1, nc - 1)),
            dma((2, nz - 1, nc - 1)),
            dma((2, nz - 1, nc)),
            dma((2, nz - 1, nc)),
            dma((2, nz, chunks)),
            dma((nz, chunks)),
            dma((2,)),
            dma((2,)),
            dma((nc - 1,)),
            dma((nc - 1,)),
            dma((nt - 1,)),
            dma((nt - 1,)),
            dma((nz - 1,)),
            dma((nz - 1,)),
        ],
        compiler_params=pltpu.CompilerParams(
            collective_id=0, has_side_effects=True, vmem_limit_bytes=56 * 2**20
        ),
    )(trajectory, initial, drive_gate, drive_candidate, gate_weight, candidate_weight)
    entries = trajectory.size * nz * nt
    residual_norm = jnp.sqrt(jnp.sum(total) / entries + 1e-06)
    return (states, residual_norm)


def solution(mesh):
    placed = (
        P("tm", None, "chan"),
        P(None, "chan"),
        P("tm", None, "chan"),
        P("tm", None, "chan"),
        P("chan", None),
        P("chan", None),
    )
    body = functools.partial(local, mesh.shape["chan"], mesh.shape["tm"])
    return jax.shard_map(
        body, mesh=mesh, in_specs=placed, out_specs=(P("tm", None, "chan"), P()), check_vma=False
    )
```

profile of v0, /device:TPU:0, one launch (start us, length us, event | category | flops | bytes accessed | tf_op | source)
XLA Modules:
  0.0 130.2 jit_solution(759785471120313028)
XLA Ops:
  0.6 123.3 %shard_map.77 = (f32[64,8,1024]{2,1,0:T(8,128)}, f32[8,128]{1,0:T(8,128)}) custom-call(f32[64,8,1024]{2,1,0:T(8,128)} %traj.1, f32[8,1024]{1,0:T(8,128)} %init.1, bf16[64,8,1024]{2,1,0:T(8,128)(2,1)} %drive_g.1, bf16[64,8,1024]{2,1,0:T(8,128)(2,1)} %drive_c.1, bf16[1024,4096]{1,0:T(8,128)(2,1)} %gate_w.1, bf16[1024,4096]{1,0:T(8,128)(2,1)} %cand_w.1), custom_call_target="tpu_custom_call" | custom-call | tf_op jit(solution)/shard_map/pallas_call | solution.py:340
  123.9 1.3 reduce_sum.9
  125.9 3.2 %copy.9 = f32[64,8,1024]{2,1,0:T(8,128)} copy(f32[64,8,1024]{2,1,0:T(8,128)} %get-tuple-element.8) | data formatting | bytes 4194304
where the time goes:
time: 130 us
  Pallas kernels  123 us (95%)
  local copies, waits for them, and re-layouts  3.16 us (2%)
  between operations  2.46 us (2%)
    pallas_call x1, Pallas kernels, local(): pl.pallas_call(functools.partial(kernel, nz, nt, chunks, tile), out_shape...  123 us
    unnamed x1, local copies, waits for them, and re-layouts  3.16 us

commit v1 on v0

v1 whole, which is shorter than its diff:
```python
import functools

import jax
import jax.numpy as jnp
from jax import lax
from jax.experimental import pallas as pl
from jax.experimental.pallas import tpu as pltpu
from jax.sharding import PartitionSpec as P

MESH = pl.DeviceIdType.MESH
BF16 = jnp.bfloat16
F32 = jnp.float32

PACED = [0.0, 9.0, 13.65, 17.0]
FIRST = [10.0, 15.5, 20.5, 26.0]
FIRST_F = [13.5, 19.0, 27.0, 36.0]
FIRST_S = [18.0, 26.0, 34.5, 43.0]
AHEAD = 12.0
ROWS = [29.0, 36.5, 42.0, 50.0, 62.0, 70.0, 77.0, 83.0]
RELAY = [31.5, 39.5, 46.0, 54.0, 66.0, 73.5, 80.0, 85.0]
QUEUE = [34.0, 57.5, 64.0, 86.0]
SUMS = [47.0, 47.1, 56.9, 57.0, 75.9, 76.0, 84.5, 93.0]
GROUPS = [(0, 2), (2, 4), (4, 6), (6, 7), (7, 8)]
NEAR = [42.5, 60.0, 68.0, 92.0]
NEXT = [(8.0, 13.0), (4.0, 8.0), (7.0, 12.0), (1.5, 3.0)]
FAR = [45.5, 63.0]
NEXT_FAR = [(7.0, 12.0), (9.0, 15.0)]
LAST = [74.0, 75.0]
NEXT_LAST = [(7.0, 11.0), (8.0, 12.0)]
WHOLE = [72.0, 80.5, 81.0, 81.5]
ADDS = [76.5, 84.0, 90.0, 90.1]
ADDS_FAR = [65.0, 84.1]
FINAL = [[91.0, 91.1, 91.2, 98.0], [95.1, 95.2, 95.3, 98.1]]


def units_of(nz):
    near, far = (4, 2) if nz <= 4 else (1, 1)
    units = [(1, d, g, p, near) for p in range(near) for g in range(2) for d in range(1, nz - 1)]
    for d in range(1, nz - 1):
        pieces = near if d == 1 else far
        units += [(0, d, g, p, pieces) for p in range(pieces) for g in range(2)]
    if nz <= 4:
        units += [(0, nz - 1, g, p, near) for p in range(near // 2, near) for g in range(2)]
    return units


def split(count):
    rows = 1
    while rows * rows * 4 <= count:
        rows *= 2
    return rows, count // rows


def kernel(
    nz, nt, chunks, tile,
    traj_in, init, drive_g_in, drive_c_in, gate_w, cand_w,
    state, prod, entry_out, total,
    guess_buf, drive_g, drive_c, wbuf, abuf, acc, sbuf,
    diag, carry, ssq, partner_map, maps, tsums, zsums,
    load_sem, local_sem, wr_send, wr_recv, cr_send, cr_recv, wz_send, wz_recv, spread_send, f_recv, s_recv, c_recv,
    a_send, a_recv, sum_send, sum_recv, row_sem, pm_sem, m_send, m_recv, ts_send, ts_recv, zs_send, zs_recv,
):
    z = lax.axis_index("chan")
    t = lax.axis_index("tm")
    steps, batch, width = traj_in.shape
    nc = nt // 2
    na, nb = split(nc)
    chip = lax.div(t, 2)
    core = lax.rem(t, 2)
    chip_a = lax.div(chip, nb)
    chip_b = lax.rem(chip, nb)
    partner = (z, t + 1 - 2 * core)
    part = width // nt
    weights = (gate_w, cand_w)
    rows = steps * batch // chunks
    chunk_steps = steps // chunks
    half = nz // 2
    units = units_of(nz)
    index = {u[:4]: n for n, u in enumerate(units)}
    count = {u[:4]: u[4] for u in units}
    lower = z < half
    s = jnp.where(lower, 1, -1)
    is_end = jnp.logical_or(z == 0, z == nz - 1)
    is_inner = jnp.logical_not(is_end)
    beside_end = jnp.logical_or(z == 1, z == nz - 2)
    end = jnp.where(lower, 0, nz - 1)

    def remote(src, dst, send, recv, device):
        return pltpu.make_async_remote_copy(
            src_ref=src, dst_ref=dst, send_sem=send, recv_sem=recv,
            device_id=device, device_id_type=MESH,
        )

    def zmod(v):
        return lax.rem(v + 2 * nz, nz)

    def cmod(v):
        return lax.rem(v + 2 * nc, nc)

    def plane_cols(k):
        return pl.ds(pl.multiple_of(k * width, 128), width)

    def piece_cols(p, pieces):
        return pl.ds(p * (width // pieces), width // pieces)

    def chip_at(g, fast, slow):
        da, db = (slow, fast) if g == 0 else (fast, slow)
        return lax.rem(chip_a + da + na, na) * nb + lax.rem(chip_b + db + nb, nb)

    def extent(g):
        return (nb, na) if g == 0 else (na, nb)

    loads = [
        pltpu.make_async_copy(traj_in, guess_buf.at[pl.ds(1, steps)], load_sem.at[0]),
        pltpu.make_async_copy(drive_g_in, drive_g, load_sem.at[1]),
        pltpu.make_async_copy(drive_c_in, drive_c, load_sem.at[2]),
    ]
    for load in loads:
        load.start()

    barrier = pltpu.get_barrier_semaphore()
    for d in range(1, nz):
        pl.semaphore_signal(barrier, inc=1, device_id=(zmod(z + d), t), device_id_type=MESH)
    for d in range(1, nt):
        pl.semaphore_signal(barrier, inc=1, device_id=(z, lax.rem(t + d, nt)), device_id_type=MESH)
    pl.semaphore_wait(barrier, nz - 1 + nt - 1)

    def row_copy():
        return remote(
            traj_in.at[steps - 1], guess_buf.at[0], row_sem.at[0], row_sem.at[1], (z, lax.rem(t + 1, nt))
        )

    def w_slot(target, g, k, p, pieces, c):
        first = pl.multiple_of(k * width + (2 * c + core) * part, 16)
        return wbuf.at[target, g, pl.ds(first, part), piece_cols(p, pieces)]

    def w_send(unit, side, method):
        target, d, g, p = unit
        n, pieces = index[unit], count[unit]
        j = zmod(z - d) if side == 0 else zmod(z + d)
        if target == 1:
            valid = j == (1 if side == 0 else nz - 2)
            out = jnp.where(side == 0, 0, nz - 1)
        elif side == 0:
            valid = jnp.logical_and(j >= 1, j < half)
            out = j
        else:
            valid = jnp.logical_and(j >= half, j <= nz - 2)
            out = j

        @pl.when(valid)
        def _():
            step = width // pieces
            src = weights[g].at[
                pl.ds(pl.multiple_of(t * part, 16), part),
                pl.ds(pl.multiple_of(out * width + p * step, 128), step),
            ]
            copy = remote(
                src, w_slot(target, g, z, p, pieces, chip), wz_send.at[side % wz_send.shape[0], n], wz_recv.at[n], (j, t)
            )
            getattr(copy, method)()

    def w_pair(unit):
        def act(method):
            for side in range(2):
                w_send(unit, side, method)

        return act

    wholes = wr_recv.shape[0]
    whole_pieces = 4

    def whole_slot(g, k, p):
        return wbuf.at[0, g, plane_cols(k), piece_cols(p, whole_pieces)]

    def whole_pair(p):
        def act(method):
            for side in range(2):
                j = zmod(z + 1) if side == 0 else zmod(z - 1)
                valid = jnp.logical_and(j >= 1, j < half) if side == 0 else jnp.logical_and(j >= half, j <= nz - 2)
                step = width // whole_pieces
                for g in range(2):
                    @pl.when(jnp.logical_and(valid, core == g))
                    def _():
                        src = weights[g].at[:, pl.ds(pl.multiple_of(j * width + p * step, 128), step)]
                        copy = remote(src, whole_slot(g, z, p), wr_send.at[side, p], wr_recv.at[p], (j, t))
                        getattr(copy, method)()

        return act

    def run(entries, depth):
        for n, entry in enumerate(entries):
            if n >= depth:
                entries[n - depth]("wait_send")
            entry("start")
        for entry in entries[max(0, len(entries) - depth):]:
            entry("wait_send")

    row_copy().start()
    ahead = 4
    deep = 64
    first_units = [u[:4] for u in units if u[0] == 1]
    groups = max(u[3] for u in first_units) + 1

    def paced_weights(p):
        first_weights(p, p + 1)

    def first_weights(low, high):
        for u in first_units:
            if low <= u[3] < high:
                w_pair(u)("start")

    first_weights(0, 1)

    def own_copy(target, g):
        out = z if target == 0 else end
        return pltpu.make_async_copy(
            weights[g].at[:, plane_cols(out)],
            wbuf.at[target, g, plane_cols(z), :],
            local_sem.at[target, g],
        )

    for g in range(2):
        own_copy(0, g).start()

    @pl.when(is_inner)
    def _():
        for g in range(2):
            @pl.when(beside_end)
            def _():
                own_copy(1, g).start()

    for g in range(2):
        own_copy(0, g).wait()
        for j in range(width // 128):
            block = wbuf[0, g, pl.ds(pl.multiple_of(z * width + j * 128, 128), 128), pl.ds(j * 128, 128)]
            eye = lax.broadcasted_iota(jnp.int32, (128, 128), 0) == lax.broadcasted_iota(
                jnp.int32, (128, 128), 1
            )
            line = jnp.sum(jnp.where(eye, block.astype(F32), 0.0), axis=0, keepdims=True)
            diag[g, :, pl.ds(j * 128, 128)] = jnp.broadcast_to(line, (batch, 128))
    loads[0].wait()

    @pl.loop(1, steps // 2)
    def _(j):
        pair = guess_buf[pl.ds(2 * j, 2)].reshape(2 * batch, width)
        abuf[pl.ds(pl.multiple_of(j * 2 * batch, 16), 2 * batch), plane_cols(z)] = pair.astype(BF16)

    row_copy().wait()

    @pl.when(t == 0)
    def _():
        guess_buf[0] = init[...]

    abuf[pl.ds(0, 2 * batch), plane_cols(z)] = guess_buf[pl.ds(0, 2)].reshape(2 * batch, width).astype(BF16)

    def a_copy(way, m, i):
        k = z - s * m
        slot = abuf.at[pl.ds(i * rows, rows), plane_cols(k)]
        to = z + s if way == 0 else z - s
        return remote(slot, slot, a_send.at[way, min(abs(m), a_send.shape[1] - 1), i], a_recv.at[k, i], (to, t))

    def sum_copy(i):
        slot = sbuf.at[:, pl.ds(i * rows, rows), :]
        return remote(slot, slot, sum_send.at[i], sum_recv.at[i], (z - s, t))

    carry[0] = jnp.ones((batch, width), F32)
    carry[1] = jnp.zeros((batch, width), F32)
    ssq[...] = jnp.zeros((batch, width), F32)

    def local_products():
        @pl.loop(0, width // tile)
        def _(n):
            cols = pl.ds(pl.multiple_of(n * tile, tile), tile)
            for g in range(2):
                acc[g, :, cols] = jnp.dot(
                    abuf[:, plane_cols(z)], wbuf[0, g, plane_cols(z), cols], preferred_element_type=F32
                )

    def accumulate(d, low, high, first, last):
        k = zmod(z + s * d)
        span = pl.ds(low * rows, (high - low) * rows)

        @pl.loop(first, last)
        def _(n):
            cols = pl.ds(pl.multiple_of(n * tile, tile), tile)
            for g in range(2):
                acc[g, span, cols] += jnp.dot(
                    abuf[span, plane_cols(k)], wbuf[0, g, plane_cols(k), cols], preferred_element_type=F32
                )

    def gates(first, length, cols, wide, gate_pre, cand_pre):
        shape = (length, batch, wide)
        span = pl.ds(first, length)
        gate_pre = gate_pre.reshape(shape) + drive_g[span, :, cols].astype(F32)
        cand_pre = cand_pre.reshape(shape) + drive_c[span, :, cols].astype(F32)
        guess = guess_buf[pl.ds(first + 1, length), :, cols]
        previous = guess_buf[span, :, cols]
        update = jax.nn.sigmoid(gate_pre)
        candidate = jnp.tanh(cand_pre)
        keep = 1.0 - update
        mapped = keep * previous + update * candidate
        jacobian = (
            keep
            + update * keep * (candidate - previous) * diag[0, :, cols][None]
            + update * (1.0 - candidate * candidate) * diag[1, :, cols][None]
        )
        offset = mapped - jacobian * previous
        missing = guess - mapped
        ssq[:, cols] += jnp.sum(missing * missing, axis=0)
        product = carry[0, :, cols]
        value = carry[1, :, cols]
        for q in range(length):
            product = jacobian[q] * product
            value = jacobian[q] * value + offset[q]
            prod[first + q, :, cols] = product
            state[first + q, :, cols] = value
        carry[0, :, cols] = product
        carry[1, :, cols] = value

    final_pieces = count[(0, 1, 0, 0)]

    @pl.when(is_end)
    def _():
        def a_entry(i):
            return lambda method: getattr(a_copy(0, 0, i), method)()

        owns = [u[:4] for u in units if u[0] == 0 and half <= u[1] < nz - 1]
        lasts = [u[:4] for u in units if u[0] == 0 and u[1] == nz - 1]
        some = (len(owns) + 1) // 2
        whole = [whole_pair(p) for p in range(wholes)]
        local_products()
        for p in range(1, groups):
            paced_weights(p)
            for u in first_units:
                if u[3] == p - 1:
                    w_pair(u)("wait_send")
        run([a_entry(i) for i in range(chunks // 2)], ahead)
        run([w_pair(u) for u in owns[:some]], ahead)
        run([a_entry(i) for i in range(chunks // 2, chunks)], ahead)
        whole[0]("start")
        run([w_pair(u) for u in owns[some:] + lasts], ahead)
        for p in range(1, wholes):
            whole[p]("start")
        for p in range(wholes):
            whole[p]("wait_send")
        for u in first_units:
            if u[3] == groups - 1:
                w_pair(u)("wait_send")
        for load in loads[1:]:
            load.wait()
        for i in range(chunks):
            sum_copy(i).wait_recv()

            @pl.loop(0, width // tile)
            def _(n):
                cols = pl.ds(pl.multiple_of(n * tile, tile), tile)
                span = pl.ds(i * rows, rows)
                gates(
                    i * chunk_steps, chunk_steps, cols, tile,
                    acc[0, span, cols] + sbuf[0, span, cols].astype(F32),
                    acc[1, span, cols] + sbuf[1, span, cols].astype(F32),
                )

    def spread(unit, arrive, df, ds, device):
        target, d, g, p = unit
        n = index[unit]
        slot = w_slot(target, g, zmod(z + s * d), p, count[unit], chip_at(g, -df, -ds))
        return remote(slot, slot, spread_send.at[n], arrive.at[n], device)

    def f_copy(unit, df):
        return spread(unit, f_recv, 0, 0, (z, 2 * chip_at(unit[2], df, 0) + core))

    def s_copy(unit, df, ds):
        return spread(unit, s_recv, df, 0, (z, 2 * chip_at(unit[2], 0, ds) + core))

    def c_copy(unit, df, ds):
        return spread(unit, c_recv, df, ds, partner)

    def parts_of(unit, arrive, parts):
        target, d, g, p = unit
        n = index[unit]
        slot = wbuf.at[target, g, pl.ds(0, parts * part), piece_cols(p, count[unit])]
        return remote(slot, slot, spread_send.at[n], arrive.at[n], partner)

    def guarded(unit, body):
        if unit[0] == 1 and nz > 4:
            pl.when(beside_end)(body)
        else:
            body()

    def z_step(unit):
        def body():
            target, d, g, p = unit
            n = index[unit]
            nf, ns = extent(g)
            slot = w_slot(target, g, zmod(z + s * d), p, count[unit], chip)
            remote(slot, slot, wz_send.at[0, n], wz_recv.at[n], partner).wait_recv()
            for df in range(1, nf):
                f_copy(unit, df).start()
            for ds in range(1, ns):
                s_copy(unit, 0, ds).start()
            c_copy(unit, 0, 0).start()

        guarded(unit, body)

    def f_step(unit):
        def body():
            nf, ns = extent(unit[2])
            if nf > 1:
                parts_of(unit, f_recv, nf - 1).wait_recv()
            for df in range(1, nf):
                for ds in range(1, ns):
                    s_copy(unit, df, ds).start()
                c_copy(unit, df, 0).start()

        guarded(unit, body)

    def s_step(unit):
        def body():
            nf, ns = extent(unit[2])
            if ns > 1:
                parts_of(unit, s_recv, nf * (ns - 1)).wait_recv()
            for df in range(nf):
                for ds in range(1, ns):
                    c_copy(unit, df, ds).start()

        guarded(unit, body)

    def c_step(unit):
        def body():
            nf, ns = extent(unit[2])
            parts_of(unit, c_recv, nf * ns).wait_recv()

        guarded(unit, body)

    def all_sends(unit):
        def body():
            nf, ns = extent(unit[2])
            parts_of(unit, c_recv, nf - 1 + nf * (ns - 1) + nf * ns).wait_send()

        guarded(unit, body)

    def within(k):
        return jnp.logical_and(k >= 0, k < nz)

    outward = jnp.logical_and(z - s >= 1, z - s <= nz - 2)

    def need(m, i):
        @pl.when(within(z + s * m))
        def _():
            a_copy(0, -m, i).wait_recv()
            if nz > 4:
                @pl.when(outward)
                def _():
                    a_copy(1, -m, i).start()

    def partial_sums(low, high):
        def body():
            depth = (nz - 1) * width
            first = pl.multiple_of(jnp.where(lower, width, 0), 128)
            span = pl.ds(low * rows, (high - low) * rows)

            @pl.loop(0, width // tile)
            def _(n):
                cols = pl.ds(pl.multiple_of(n * tile, tile), tile)
                lhs = abuf[span, pl.ds(first, depth)]
                for g in range(2):
                    sbuf[g, span, cols] = jnp.dot(
                        lhs, wbuf[1, g, pl.ds(first, depth), cols], preferred_element_type=F32
                    ).astype(BF16)

            for i in range(low, high):
                sum_copy(i).start()

        if nz > 4:
            pl.when(beside_end)(body)
        else:
            body()

    def final(p, h):
        k = zmod(z + s)
        wide = width // final_pieces
        long = rows * 2

        @pl.loop(h * (chunks // 4), (h + 1) * (chunks // 4))
        def _(r):
            span = pl.ds(pl.multiple_of(r * long, long), long)
            for n in range(wide // min(tile, wide)):
                step = min(tile, wide)
                cols = pl.ds(p * wide + n * step, step)
                pre = [
                    acc[g, span, cols]
                    + jnp.dot(
                        abuf[span, plane_cols(k)], wbuf[0, g, plane_cols(k), cols], preferred_element_type=F32
                    )
                    for g in range(2)
                ]
                gates(r * (long // batch), long // batch, cols, step, *pre)

    def setup_end():
        def body():
            for g in range(2):
                own_copy(1, g).wait()

        if nz > 4:
            pl.when(beside_end)(body)
        else:
            body()

    def whole_step(p):
        k = zmod(z - s)
        for g in range(2):
            @pl.when(core == g)
            def _():
                slot = whole_slot(g, k, p)
                remote(slot, slot, wr_send.at[0, p], wr_recv.at[p], partner).wait_recv()
                remote(slot, slot, cr_send.at[p], cr_recv.at[p], partner).start()

    def whole_arrive(p):
        slot = whole_slot(0, zmod(z - s), p)
        remote(slot, slot, cr_send.at[p], cr_recv.at[p], partner).wait_recv()

    def whole_done(p):
        slot = whole_slot(0, zmod(z - s), p)
        remote(slot, slot, cr_send.at[p], cr_recv.at[p], partner).wait_send()

    events = []

    def at(time, body, *args):
        events.append((time, len(events), body, args))

    def w_entry(unit):
        return w_pair(unit)

    def rows_entry(i):
        def act(method):
            getattr(a_copy(0, 0, i), method)()
            if nz > 4:
                @pl.when(outward)
                def _():
                    getattr(a_copy(1, 0, i), method)()

        return act

    def relay_entry(m, i):
        def act(method):
            @pl.when(within(z - s * m))
            def _():
                if method == "start":
                    a_copy(0, m, i).wait_recv()
                getattr(a_copy(0, m, i), method)()

        return act

    queue = []

    def push(entry, done):
        queue.append((entry, done))

    def pump(n):
        if n >= deep:
            queue[n - deep][0]("wait_send")
        queue[n][0]("start")

    ends = [u[:4] for u in units if u[0] == 1]
    owns = [u[:4] for u in units if u[0] == 0]
    for u in ends:
        target, d, g, p = u
        e = 4 * p // groups if groups >= 4 else p
        at(FIRST[e] + 0.1 * d, z_step, u)
        at(FIRST_F[e] + 0.1 * d, f_step, u)
        at(FIRST_S[e] + 0.1 * d, s_step, u)
        at(SUMS[0] - 0.5, c_step, u)
        at(SUMS[0] + 10.0, all_sends, u)
    begun = 0
    for p in range(1, groups):
        at(PACED[p % 4], paced_weights, p)

    def last_paced():
        for u in first_units:
            w_pair(u)("wait_send")

    at(60.0, last_paced)
    for i in range(chunks):
        push(rows_entry(i), ROWS[i])
        for m in range(1, half):
            push(relay_entry(m, i), RELAY[i] + 0.01 * m)
        for m in range(1, nz - 1):
            at(SUMS[i] + 0.01 * m, need, m, i)
    for low, high in GROUPS:
        at(SUMS[high - 1] + 0.2, partial_sums, low, high)
    for u in owns:
        target, d, g, p = u
        if d == 1:
            push(w_entry(u), QUEUE[p] + 0.5 * g)
            done = NEAR[p] + 0.5 * g
        elif d == nz - 1:
            done = LAST[p - 2] + 0.5 * g
        else:
            done = FAR[p] + 3.0 * g + 0.1 * d
            if nz > 4:
                push(w_entry(u), 30.0 + 0.1 * d)
        after = NEXT[p] if d == 1 else NEXT_LAST[p - 2] if d == nz - 1 else NEXT_FAR[p]
        at(done, z_step, u)
        at(done + after[0], f_step, u)
        at(done + after[1], s_step, u)
        at(done + after[1] + (2.0 if done < 90.0 else 1.0), c_step, u)
    queue.sort(key=lambda entry: entry[1])
    previous_time = 0.0
    for n in range(begun, len(queue)):
        previous_time = max(previous_time + 0.001, queue[n][1] - AHEAD, 18.5)
        at(previous_time, pump, n)
    for p in range(wholes):
        at(WHOLE[p], whole_step, p)
        at(WHOLE[p] + 3.0, whole_arrive, p)

    tiles = width // tile
    if nz > 4:
        for p in range(wholes):
            at(26.0, whole_pair(p), "start")
    at(4.0, local_products)
    at(4.1, setup_end)
    if nz == 4:
        middle = chunks // 2
        for h in range(2):
            at(ADDS_FAR[h], accumulate, 2, 0, middle, h * tiles // 2, (h + 1) * tiles // 2)
        at(SUMS[7] + 1.0, accumulate, 2, middle, chunks, 0, tiles)
        for p in range(4):
            at(ADDS[p], accumulate, 3, 0, chunks, p * tiles // 4, (p + 1) * tiles // 4)
    else:
        for d in range(2, nz):
            at(98.0 + 0.1 * d, accumulate, d, 0, chunks, 0, tiles)
    for load in loads[1:]:
        at(20.0, load.wait)
    for p in range(final_pieces):
        for h in range(2):
            at(FINAL[h][p] if nz == 4 else 99.0 + 0.1 * h + 0.01 * p, final, p, h)

    @pl.when(is_inner)
    def _():
        for _, _, body, args in sorted(events, key=lambda event: event[:2]):
            body(*args)

    def pm_copy():
        return remote(carry, partner_map, pm_sem.at[0], pm_sem.at[1], partner)

    pm_copy().start()
    mine = ssq[:, pl.ds(0, 128)]
    for j in range(1, width // 128):
        mine = mine + ssq[:, pl.ds(j * 128, 128)]
    tsums[t] = mine

    def ts_copy(d):
        slot = tsums.at[t]
        return remote(slot, slot, ts_send.at[d - 1], ts_recv.at[d - 1], (z, lax.rem(t + d, nt)))

    def ts_arrival(d):
        slot = tsums.at[lax.rem(t + nt - d, nt)]
        return remote(slot, slot, ts_send.at[d - 1], ts_recv.at[d - 1], partner)

    for d in range(1, nt):
        ts_copy(d).start()

    def m_copy(dq):
        slot = maps.at[chip]
        return remote(
            slot, slot, m_send.at[dq - 1], m_recv.at[dq - 1], (z, 2 * cmod(chip + dq) + core)
        )

    def m_arrival(dq):
        slot = maps.at[cmod(chip - dq)]
        return remote(slot, slot, m_send.at[dq - 1], m_recv.at[dq - 1], partner)

    pm_copy().wait()
    is_second = core == 1
    p_mine, s_mine, p_other, s_other = carry[0], carry[1], partner_map[0], partner_map[1]
    p_late = jnp.where(is_second, p_mine, p_other)
    s_early = jnp.where(is_second, s_other, s_mine)
    s_late = jnp.where(is_second, s_mine, s_other)
    maps[chip, 0] = p_mine * p_other
    maps[chip, 1] = p_late * s_early + s_late
    for dq in range(1, nc):
        m_copy(dq).start()

    @pl.when(is_inner)
    def _():
        for u in owns:
            all_sends(u)
        for entry, _ in queue[max(0, len(queue) - deep):]:
            entry("wait_send")
        for p in range(wholes):
            whole_done(p)
            if nz > 4:
                whole_pair(p)("wait_send")
        for i in range(chunks):
            if nz > 4:
                @pl.when(outward)
                def _():
                    for m in range(1, nz - 1):
                        @pl.when(within(z + s * m))
                        def _():
                            a_copy(1, -m, i).wait_send()

            @pl.when(beside_end)
            def _():
                sum_copy(i).wait_send()

    for d in range(1, nt):
        ts_arrival(d).wait_recv()
    plane = tsums[0]
    for k in range(1, nt):
        plane = plane + tsums[k]
    zsums[z] = plane

    def zs_copy(d):
        slot = zsums.at[z]
        return remote(slot, slot, zs_send.at[d - 1], zs_recv.at[d - 1], (zmod(z + d), t))

    def zs_arrival(d):
        slot = zsums.at[zmod(z - d)]
        return remote(slot, slot, zs_send.at[d - 1], zs_recv.at[d - 1], partner)

    for d in range(1, nz):
        zs_copy(d).start()

    for dq in range(1, nc):
        m_arrival(dq).wait_recv()
    entry = init[...]
    for q in range(nc):
        entry = jnp.where(q < chip, maps[q, 0] * entry + maps[q, 1], entry)
    entry_out[...] = jnp.where(is_second, p_other * entry + s_other, entry)

    for d in range(1, nt):
        ts_copy(d).wait_send()
    for dq in range(1, nc):
        m_copy(dq).wait_send()
    for d in range(1, nz):
        zs_arrival(d).wait_recv()
    whole = zsums[0]
    for k in range(1, nz):
        whole = whole + zsums[k]
    total[...] = whole
    for d in range(1, nz):
        zs_copy(d).wait_send()


def finish(entries, state, prod, entry, total, states, norm, held, out_sem):
    parts = out_sem.shape[0]
    span = state.shape[0] // parts

    def put(n):
        return pltpu.make_async_copy(
            held.at[pl.ds(n * span, span)], states.at[pl.ds(n * span, span)], out_sem.at[n]
        )

    for n in range(parts):
        @pl.loop(n * span, (n + 1) * span)
        def _(q):
            held[q] = prod[q] * entry[...] + state[q]

        put(n).start()
    line = jnp.sum(total[...], axis=0, keepdims=True)
    norm[...] = jnp.sqrt(jnp.sum(line, axis=1, keepdims=True) / entries + 1e-06)
    for n in range(parts):
        put(n).wait()


def local(nz, nt, trajectory, initial, drive_gate, drive_candidate, gate_weight, candidate_weight):
    steps, batch, width = trajectory.shape
    nc = nt // 2
    full = gate_weight.shape[1]
    chunks = 8
    parts = 8
    tile = min(256, width)
    units = len(units_of(nz))
    pieces = 2 if nz == 4 else 4
    ways = 1 if nz == 4 else 2
    entries = trajectory.size * nz * nt
    dma = pltpu.SemaphoreType.DMA
    vmem = pl.BlockSpec(memory_space=pltpu.VMEM)
    hbm = pl.BlockSpec(memory_space=pltpu.HBM)
    block = (steps, batch, width)
    state, prod, entry, total = pl.pallas_call(
        functools.partial(kernel, nz, nt, chunks, tile),
        out_shape=(
            pltpu.VMEM(block, F32),
            pltpu.VMEM(block, F32),
            pltpu.VMEM((batch, width), F32),
            pltpu.VMEM((batch, 128), F32),
        ),
        in_specs=[hbm, vmem, hbm, hbm, hbm, hbm],
        out_specs=(vmem, vmem, vmem, vmem),
        scratch_shapes=[
            pltpu.VMEM((steps + 1, batch, width), F32),
            pltpu.VMEM(block, BF16),
            pltpu.VMEM(block, BF16),
            pltpu.VMEM((2, 2, full, width), BF16),
            pltpu.VMEM((steps * batch, full), BF16),
            pltpu.VMEM((2, steps * batch, width), F32),
            pltpu.VMEM((2, steps * batch, width), BF16),
            pltpu.VMEM((2, batch, width), F32),
            pltpu.VMEM((2, batch, width), F32),
            pltpu.VMEM((batch, width), F32),
            pltpu.VMEM((2, batch, width), F32),
            pltpu.VMEM((nc, 2, batch, width), F32),
            pltpu.VMEM((nt, batch, 128), F32),
            pltpu.VMEM((nz, batch, 128), F32),
            dma((3,)),
            dma((2, 2)),
            dma((2, pieces)),
            dma((pieces,)),
            dma((pieces,)),
            dma((pieces,)),
            dma((ways, units)),
            dma((units,)),
            dma((units,)),
            dma((units,)),
            dma((units,)),
            dma((units,)),
            dma((ways, nz // 2 if ways == 1 else nz, chunks)),
            dma((nz, chunks)),
            dma((chunks,)),
            dma((chunks,)),
            dma((2,)),
            dma((2,)),
            dma((nc - 1,)),
            dma((nc - 1,)),
            dma((nt - 1,)),
            dma((nt - 1,)),
            dma((nz - 1,)),
            dma((nz - 1,)),
        ],
        compiler_params=pltpu.CompilerParams(
            collective_id=0, has_side_effects=True, vmem_limit_bytes=56 * 2**20
        ),
    )(*(
        pltpu.with_memory_space_constraint(x, pltpu.HBM) if x.ndim == 3 or x.shape[1] == full else x
        for x in (trajectory, initial, drive_gate, drive_candidate, gate_weight, candidate_weight)
    ))
    states, norm = pl.pallas_call(
        functools.partial(finish, entries),
        out_shape=(jax.ShapeDtypeStruct(block, F32), jax.ShapeDtypeStruct((1, 1), F32)),
        in_specs=[vmem, vmem, vmem, vmem],
        out_specs=(hbm, vmem),
        scratch_shapes=[pltpu.VMEM(block, F32), dma((parts,))],
        compiler_params=pltpu.CompilerParams(vmem_limit_bytes=8 * 2**20),
    )(state, prod, entry, total)
    return (states, norm.reshape(()))


def solution(mesh):
    placed = (
        P("tm", None, "chan"),
        P(None, "chan"),
        P("tm", None, "chan"),
        P("tm", None, "chan"),
        P("chan", None),
        P("chan", None),
    )
    body = functools.partial(local, mesh.shape["chan"], mesh.shape["tm"])
    return jax.shard_map(
        body, mesh=mesh, in_specs=placed, out_specs=(P("tm", None, "chan"), P()), check_vma=False
    )
```

time: 130 us -> 128 us (0.985)
  Pallas kernels: 123 us -> 128 us
  local copies, waits for them, and re-layouts: 3.16 us -> 0 us
  between operations: 2.46 us -> 0.64 us
    unnamed x1 -> x0, local copies, waits for them, and re-layouts: 3.16 us -> none
    pallas_call x1, Pallas kernels: 123 us -> 126 us  [local(): pl.pallas_call(functools.partial(kernel, nz, nt, chunks, tile), out_shape...]
    pallas_call x0 -> x1, Pallas kernels: none -> 1.94 us  [local(): pl.pallas_call(functools.partial(finish, entries), out_shape=(jax.ShapeDt...]
where the time goes in v1:
time: 128 us
  Pallas kernels  128 us (100%)
    pallas_call x1, Pallas kernels, local(): pl.pallas_call(functools.partial(kernel, nz, nt, chunks, tile), out_shape...  126 us

profile of v1, /device:TPU:0, one launch (start us, length us, event | category | flops | bytes accessed | tf_op | source)
XLA Modules:
  0.0 128.2 jit_solution(14366788152716869720)
XLA Ops:
  0.6 125.6 %shard_map.77 = (f32[64,8,1024]{2,1,0:T(8,128)S(1)}, f32[64,8,1024]{2,1,0:T(8,128)S(1)}, f32[8,1024]{1,0:T(8,128)S(1)}, f32[8,128]{1,0:T(8,128)S(1)}) custom-call(f32[64,8,1024]{2,1,0:T(8,128)} %traj_in.1, f32[8,1024]{1,0:T(8,128)} %init.1, bf16[64,8,1024]{2,1,0:T(8,128)(2,1)} %drive_g_in.1, bf16[64,8,1024]{2,1,0:T(8,128)(2,1)} %drive_c_in.1, ...), custom_call_target="tpu_custom_call" | custom-call | tf_op jit(solution)/shard_map/pallas_call | solution.py:784
  126.2 1.9 %shard_map.78 = (f32[64,8,1024]{2,1,0:T(8,128)}, f32[1,1]{1,0:T(1,128)}) custom-call(f32[64,8,1024]{2,1,0:T(8,128)S(1)} %get-tuple-element.8.state, f32[64,8,1024]{2,1,0:T(8,128)S(1)} %get-tuple-element.9.prod, f32[8,1024]{1,0:T(8,128)S(1)} %get-tuple-element.10.entry, f32[8,128]{1,0:T(8,128)S(1)} %get-tuple-element.11.total), custom_call_target="tpu_custom_call" | custom-call | tf_op jit(solution)/shard_map/pallas_call | solution.py:841

commit v2 on v1

--- a/solution.py
+++ b/solution.py
@@ -15,22 +15,23 @@
 FIRST = [10.0, 15.5, 20.5, 26.0]
 FIRST_F = [13.5, 19.0, 27.0, 36.0]
 FIRST_S = [18.0, 26.0, 34.5, 43.0]
+LOCAL = [25.5, 34.4, 36.5, 42.9]
 AHEAD = 12.0
-ROWS = [29.0, 36.5, 42.0, 50.0, 62.0, 70.0, 77.0, 83.0]
-RELAY = [31.5, 39.5, 46.0, 54.0, 66.0, 73.5, 80.0, 85.0]
-QUEUE = [34.0, 57.5, 64.0, 86.0]
-SUMS = [47.0, 47.1, 56.9, 57.0, 75.9, 76.0, 84.5, 93.0]
-GROUPS = [(0, 2), (2, 4), (4, 6), (6, 7), (7, 8)]
-NEAR = [42.5, 60.0, 68.0, 92.0]
-NEXT = [(8.0, 13.0), (4.0, 8.0), (7.0, 12.0), (1.5, 3.0)]
+ROWS = [28.0, 36.0, 40.0, 48.0, 59.0, 64.0, 72.0, 78.0]
+RELAY = [30.5, 38.0, 43.0, 51.0, 61.5, 66.0, 75.0, 81.0]
+QUEUE = [33.0, 46.0, 68.0, 77.0]
+SUMS = [47.0, 47.1, 58.5, 66.5, 71.5, 77.5, 84.0, 90.0]
+GROUPS = [(0, 2), (2, 3), (3, 4), (4, 5), (5, 6), (6, 7), (7, 8)]
+NEAR = [42.5, 53.0, 74.0, 86.0]
+NEXT = [(8.0, 12.0), (8.0, 12.0), (6.5, 11.0), (4.5, 7.5)]
 FAR = [45.5, 63.0]
-NEXT_FAR = [(7.0, 12.0), (9.0, 15.0)]
-LAST = [74.0, 75.0]
-NEXT_LAST = [(7.0, 11.0), (8.0, 12.0)]
-WHOLE = [72.0, 80.5, 81.0, 81.5]
-ADDS = [76.5, 84.0, 90.0, 90.1]
-ADDS_FAR = [65.0, 84.1]
-FINAL = [[91.0, 91.1, 91.2, 98.0], [95.1, 95.2, 95.3, 98.1]]
+NEXT_FAR = [(9.0, 14.5), (6.0, 12.0)]
+LAST = [71.0]
+NEXT_LAST = [(7.0, 12.5)]
+WHOLE = [70.5, 77.5, 87.6, 88.0]
+ADDS = [74.0, 81.0, 91.0, 88.6]
+SPANS = [(0, 4), (4, 6), (6, 8)]
+FINAL = [[74.2, 81.1, 91.1, 96.2], [81.2, 81.3, 91.2, 96.3], [92.0, 92.4, 92.5, 96.4]]
 
 
 def units_of(nz):
@@ -40,7 +41,7 @@
         pieces = near if d == 1 else far
         units += [(0, d, g, p, pieces) for p in range(pieces) for g in range(2)]
     if nz <= 4:
-        units += [(0, nz - 1, g, p, near) for p in range(near // 2, near) for g in range(2)]
+        units += [(0, nz - 1, g, p, near) for p in range(near - 1, near) for g in range(2)]
     return units
 
 
@@ -55,7 +56,7 @@
     nz, nt, chunks, tile,
     traj_in, init, drive_g_in, drive_c_in, gate_w, cand_w,
     state, prod, entry_out, total,
-    guess_buf, drive_g, drive_c, wbuf, abuf, acc, sbuf,
+    guess_buf, drive_g, drive_c, wbuf, abuf, acc, end_acc, sbuf,
     diag, carry, ssq, partner_map, maps, tsums, zsums,
     load_sem, local_sem, wr_send, wr_recv, cr_send, cr_recv, wz_send, wz_recv, spread_send, f_recv, s_recv, c_recv,
     a_send, a_recv, sum_send, sum_recv, row_sem, pm_sem, m_send, m_recv, ts_send, ts_recv, zs_send, zs_recv,
@@ -455,10 +456,25 @@
                 def _():
                     a_copy(1, -m, i).start()
 
+    def local_sums(first, last):
+        def body():
+            @pl.loop(first, last)
+            def _(n):
+                cols = pl.ds(pl.multiple_of(n * tile, tile), tile)
+                for g in range(2):
+                    end_acc[g, :, cols] = jnp.dot(
+                        abuf[:, plane_cols(z)], wbuf[1, g, plane_cols(z), cols], preferred_element_type=F32
+                    )
+
+        if nz > 4:
+            pl.when(beside_end)(body)
+        else:
+            body()
+
     def partial_sums(low, high):
         def body():
-            depth = (nz - 1) * width
-            first = pl.multiple_of(jnp.where(lower, width, 0), 128)
+            depth = (nz - 2) * width
+            first = pl.multiple_of(jnp.where(lower, 2 * width, 0), 128)
             span = pl.ds(low * rows, (high - low) * rows)
 
             @pl.loop(0, width // tile)
@@ -466,8 +482,9 @@
                 cols = pl.ds(pl.multiple_of(n * tile, tile), tile)
                 lhs = abuf[span, pl.ds(first, depth)]
                 for g in range(2):
-                    sbuf[g, span, cols] = jnp.dot(
-                        lhs, wbuf[1, g, pl.ds(first, depth), cols], preferred_element_type=F32
+                    sbuf[g, span, cols] = (
+                        end_acc[g, span, cols]
+                        + jnp.dot(lhs, wbuf[1, g, pl.ds(first, depth), cols], preferred_element_type=F32)
                     ).astype(BF16)
 
             for i in range(low, high):
@@ -478,24 +495,26 @@
         else:
             body()
 
-    def final(p, h):
-        k = zmod(z + s)
+    def final(p, low, high):
+        blocks = [zmod(z + s * d) for d in ((1, 2) if nz == 4 else (1,))]
         wide = width // final_pieces
         long = rows * 2
 
-        @pl.loop(h * (chunks // 4), (h + 1) * (chunks // 4))
+        @pl.loop(low // 2, high // 2)
         def _(r):
             span = pl.ds(pl.multiple_of(r * long, long), long)
             for n in range(wide // min(tile, wide)):
                 step = min(tile, wide)
                 cols = pl.ds(p * wide + n * step, step)
-                pre = [
-                    acc[g, span, cols]
-                    + jnp.dot(
-                        abuf[span, plane_cols(k)], wbuf[0, g, plane_cols(k), cols], preferred_element_type=F32
-                    )
-                    for g in range(2)
-                ]
+                pre = []
+                for g in range(2):
+                    sums = acc[g, span, cols]
+                    for k in blocks:
+                        sums += jnp.dot(
+                            abuf[span, plane_cols(k)], wbuf[0, g, plane_cols(k), cols],
+                            preferred_element_type=F32,
+                        )
+                    pre.append(sums)
                 gates(r * (long // batch), long // batch, cols, step, *pre)
 
     def setup_end():
@@ -596,12 +615,12 @@
             push(w_entry(u), QUEUE[p] + 0.5 * g)
             done = NEAR[p] + 0.5 * g
         elif d == nz - 1:
-            done = LAST[p - 2] + 0.5 * g
+            done = LAST[0] + 0.5 * g
         else:
             done = FAR[p] + 3.0 * g + 0.1 * d
             if nz > 4:
                 push(w_entry(u), 30.0 + 0.1 * d)
-        after = NEXT[p] if d == 1 else NEXT_LAST[p - 2] if d == nz - 1 else NEXT_FAR[p]
+        after = NEXT[p] if d == 1 else NEXT_LAST[0] if d == nz - 1 else NEXT_FAR[p]
         at(done, z_step, u)
         at(done + after[0], f_step, u)
         at(done + after[1], s_step, u)
@@ -622,20 +641,19 @@
     at(4.0, local_products)
     at(4.1, setup_end)
     if nz == 4:
-        middle = chunks // 2
-        for h in range(2):
-            at(ADDS_FAR[h], accumulate, 2, 0, middle, h * tiles // 2, (h + 1) * tiles // 2)
-        at(SUMS[7] + 1.0, accumulate, 2, middle, chunks, 0, tiles)
+        for n in range(tiles):
+            at(LOCAL[n], local_sums, n, n + 1)
         for p in range(4):
             at(ADDS[p], accumulate, 3, 0, chunks, p * tiles // 4, (p + 1) * tiles // 4)
     else:
+        at(4.3, local_sums, 0, tiles)
         for d in range(2, nz):
             at(98.0 + 0.1 * d, accumulate, d, 0, chunks, 0, tiles)
     for load in loads[1:]:
         at(20.0, load.wait)
     for p in range(final_pieces):
-        for h in range(2):
-            at(FINAL[h][p] if nz == 4 else 99.0 + 0.1 * h + 0.01 * p, final, p, h)
+        for h, (low, high) in enumerate(SPANS):
+            at(FINAL[h][p] if nz == 4 else 99.0 + 0.1 * h + 0.01 * p, final, p, low, high)
 
     @pl.when(is_inner)
     def _():
@@ -774,7 +792,7 @@
     parts = 8
     tile = min(256, width)
     units = len(units_of(nz))
-    pieces = 2 if nz == 4 else 4
+    pieces = 3 if nz == 4 else 4
     ways = 1 if nz == 4 else 2
     entries = trajectory.size * nz * nt
     dma = pltpu.SemaphoreType.DMA
@@ -797,6 +815,7 @@
             pltpu.VMEM(block, BF16),
             pltpu.VMEM((2, 2, full, width), BF16),
             pltpu.VMEM((steps * batch, full), BF16),
+            pltpu.VMEM((2, steps * batch, width), F32),
             pltpu.VMEM((2, steps * batch, width), F32),
             pltpu.VMEM((2, steps * batch, width), BF16),
             pltpu.VMEM((2, batch, width), F32),

time: 128 us -> 119 us (0.930)
  Pallas kernels: 128 us -> 118 us
    pallas_call x1, Pallas kernels: 126 us -> 116 us  [local(): pl.pallas_call(functools.partial(kernel, nz, nt, chunks, tile), out_shape...]
where the time goes in v2:
time: 119 us
  Pallas kernels  118 us (99%)
    pallas_call x1, Pallas kernels, local(): pl.pallas_call(functools.partial(kernel, nz, nt, chunks, tile), out_shape...  116 us

profile of v2, /device:TPU:0, one launch (start us, length us, event | category | flops | bytes accessed | tf_op | source)
XLA Modules:
  0.0 119.0 jit_solution(8001612890340616576)
XLA Ops:
  0.6 116.4 %shard_map.77 = (f32[64,8,1024]{2,1,0:T(8,128)S(1)}, f32[64,8,1024]{2,1,0:T(8,128)S(1)}, f32[8,1024]{1,0:T(8,128)S(1)}, f32[8,128]{1,0:T(8,128)S(1)}) custom-call(f32[64,8,1024]{2,1,0:T(8,128)} %traj_in.1, f32[8,1024]{1,0:T(8,128)} %init.1, bf16[64,8,1024]{2,1,0:T(8,128)(2,1)} %drive_g_in.1, bf16[64,8,1024]{2,1,0:T(8,128)(2,1)} %drive_c_in.1, ...), custom_call_target="tpu_custom_call" | custom-call | tf_op jit(solution)/shard_map/pallas_call | solution.py:802
  117.1 1.9 %shard_map.78 = (f32[64,8,1024]{2,1,0:T(8,128)}, f32[1,1]{1,0:T(1,128)}) custom-call(f32[64,8,1024]{2,1,0:T(8,128)S(1)} %get-tuple-element.8.state, f32[64,8,1024]{2,1,0:T(8,128)S(1)} %get-tuple-element.9.prod, f32[8,1024]{1,0:T(8,128)S(1)} %get-tuple-element.10.entry, f32[8,128]{1,0:T(8,128)S(1)} %get-tuple-element.11.total), custom_call_target="tpu_custom_call" | custom-call | tf_op jit(solution)/shard_map/pallas_call | solution.py:860

commit v3 on v2

--- a/solution.py
+++ b/solution.py
@@ -17,21 +17,22 @@
 FIRST_S = [18.0, 26.0, 34.5, 43.0]
 LOCAL = [25.5, 34.4, 36.5, 42.9]
 AHEAD = 12.0
-ROWS = [28.0, 36.0, 40.0, 48.0, 59.0, 64.0, 72.0, 78.0]
-RELAY = [30.5, 38.0, 43.0, 51.0, 61.5, 66.0, 75.0, 81.0]
-QUEUE = [33.0, 46.0, 68.0, 77.0]
-SUMS = [47.0, 47.1, 58.5, 66.5, 71.5, 77.5, 84.0, 90.0]
+AFTER = 3.0
+ROWS = [28.0, 36.0, 40.0, 48.0, 59.0, 64.0, 72.0, 77.0]
+RELAY = [30.5, 38.0, 43.0, 51.0, 61.5, 66.0, 74.0, 80.0]
+QUEUE = [33.0, 46.0, 63.0, 75.5]
+SUMS = [47.0, 47.1, 58.5, 66.5, 71.5, 77.5, 81.0, 88.4]
 GROUPS = [(0, 2), (2, 3), (3, 4), (4, 5), (5, 6), (6, 7), (7, 8)]
-NEAR = [42.5, 53.0, 74.0, 86.0]
-NEXT = [(8.0, 12.0), (8.0, 12.0), (6.5, 11.0), (4.5, 7.5)]
+NEAR = [42.5, 53.0, 74.3, 83.0]
+NEXT = [(8.0, 12.0), (8.0, 12.0), (5.2, 8.0), (4.8, 6.2)]
 FAR = [45.5, 63.0]
 NEXT_FAR = [(9.0, 14.5), (6.0, 12.0)]
-LAST = [71.0]
-NEXT_LAST = [(7.0, 12.5)]
-WHOLE = [70.5, 77.5, 87.6, 88.0]
-ADDS = [74.0, 81.0, 91.0, 88.6]
+LAST = [71.0, 71.1]
+NEXT_LAST = [(7.0, 12.5), (7.1, 12.6)]
+WHOLE = [70.5, 76.9, 84.3, 84.4]
+ADDS = [74.0, 80.0, 87.3, 87.35]
 SPANS = [(0, 4), (4, 6), (6, 8)]
-FINAL = [[74.2, 81.1, 91.1, 96.2], [81.2, 81.3, 91.2, 96.3], [92.0, 92.4, 92.5, 96.4]]
+FINAL = [[74.2, 80.1, 87.5, 96.2], [80.2, 80.3, 89.75, 96.3], [89.8, 89.9, 90.0, 96.4]]
 
 
 def units_of(nz):
@@ -41,7 +42,7 @@
         pieces = near if d == 1 else far
         units += [(0, d, g, p, pieces) for p in range(pieces) for g in range(2)]
     if nz <= 4:
-        units += [(0, nz - 1, g, p, near) for p in range(near - 1, near) for g in range(2)]
+        units += [(0, nz - 1, g, p, near) for p in range(near // 2, near) for g in range(2)]
     return units
 
 
@@ -74,7 +75,7 @@
     part = width // nt
     weights = (gate_w, cand_w)
     rows = steps * batch // chunks
-    chunk_steps = steps // chunks
+    cuts = [(i * rows, rows) for i in range(chunks)]
     half = nz // 2
     units = units_of(nz)
     index = {u[:4]: n for n, u in enumerate(units)}
@@ -257,13 +258,13 @@
 
     def a_copy(way, m, i):
         k = z - s * m
-        slot = abuf.at[pl.ds(i * rows, rows), plane_cols(k)]
+        slot = abuf.at[pl.ds(*cuts[i]), plane_cols(k)]
         to = z + s if way == 0 else z - s
         return remote(slot, slot, a_send.at[way, min(abs(m), a_send.shape[1] - 1), i], a_recv.at[k, i], (to, t))
 
-    def sum_copy(i):
-        slot = sbuf.at[:, pl.ds(i * rows, rows), :]
-        return remote(slot, slot, sum_send.at[i], sum_recv.at[i], (z - s, t))
+    def sum_copy(i, h):
+        slot = sbuf.at[:, pl.ds(*cuts[i]), piece_cols(h, 2)]
+        return remote(slot, slot, sum_send.at[2 * i + h], sum_recv.at[2 * i + h], (z - s, t))
 
     carry[0] = jnp.ones((batch, width), F32)
     carry[1] = jnp.zeros((batch, width), F32)
@@ -338,7 +339,7 @@
                     w_pair(u)("wait_send")
         run([a_entry(i) for i in range(chunks // 2)], ahead)
         run([w_pair(u) for u in owns[:some]], ahead)
-        run([a_entry(i) for i in range(chunks // 2, chunks)], ahead)
+        run([a_entry(i) for i in range(chunks // 2, len(cuts))], ahead)
         whole[0]("start")
         run([w_pair(u) for u in owns[some:] + lasts], ahead)
         for p in range(1, wholes):
@@ -350,15 +351,16 @@
                 w_pair(u)("wait_send")
         for load in loads[1:]:
             load.wait()
-        for i in range(chunks):
-            sum_copy(i).wait_recv()
-
-            @pl.loop(0, width // tile)
+        half_tiles = width // tile // 2
+        for i, h in [(i, h) for i in range(len(cuts)) for h in range(2)]:
+            sum_copy(i, h).wait_recv()
+
+            @pl.loop(h * half_tiles, (h + 1) * half_tiles)
             def _(n):
                 cols = pl.ds(pl.multiple_of(n * tile, tile), tile)
-                span = pl.ds(i * rows, rows)
+                span = pl.ds(*cuts[i])
                 gates(
-                    i * chunk_steps, chunk_steps, cols, tile,
+                    cuts[i][0] // batch, cuts[i][1] // batch, cols, tile,
                     acc[0, span, cols] + sbuf[0, span, cols].astype(F32),
                     acc[1, span, cols] + sbuf[1, span, cols].astype(F32),
                 )
@@ -475,20 +477,22 @@
         def body():
             depth = (nz - 2) * width
             first = pl.multiple_of(jnp.where(lower, 2 * width, 0), 128)
-            span = pl.ds(low * rows, (high - low) * rows)
-
-            @pl.loop(0, width // tile)
-            def _(n):
-                cols = pl.ds(pl.multiple_of(n * tile, tile), tile)
-                lhs = abuf[span, pl.ds(first, depth)]
-                for g in range(2):
-                    sbuf[g, span, cols] = (
-                        end_acc[g, span, cols]
-                        + jnp.dot(lhs, wbuf[1, g, pl.ds(first, depth), cols], preferred_element_type=F32)
-                    ).astype(BF16)
-
-            for i in range(low, high):
-                sum_copy(i).start()
+            span = pl.ds(cuts[low][0], sum(cut[1] for cut in cuts[low:high]))
+
+            half_tiles = width // tile // 2
+            for h in range(2):
+                @pl.loop(h * half_tiles, (h + 1) * half_tiles)
+                def _(n):
+                    cols = pl.ds(pl.multiple_of(n * tile, tile), tile)
+                    lhs = abuf[span, pl.ds(first, depth)]
+                    for g in range(2):
+                        sbuf[g, span, cols] = (
+                            end_acc[g, span, cols]
+                            + jnp.dot(lhs, wbuf[1, g, pl.ds(first, depth), cols], preferred_element_type=F32)
+                        ).astype(BF16)
+
+                for i in range(low, high):
+                    sum_copy(i, h).start()
 
         if nz > 4:
             pl.when(beside_end)(body)
@@ -601,7 +605,7 @@
             w_pair(u)("wait_send")
 
     at(60.0, last_paced)
-    for i in range(chunks):
+    for i in range(len(cuts)):
         push(rows_entry(i), ROWS[i])
         for m in range(1, half):
             push(relay_entry(m, i), RELAY[i] + 0.01 * m)
@@ -615,16 +619,16 @@
             push(w_entry(u), QUEUE[p] + 0.5 * g)
             done = NEAR[p] + 0.5 * g
         elif d == nz - 1:
-            done = LAST[0] + 0.5 * g
+            done = LAST[p - 2] + 0.5 * g
         else:
             done = FAR[p] + 3.0 * g + 0.1 * d
             if nz > 4:
                 push(w_entry(u), 30.0 + 0.1 * d)
-        after = NEXT[p] if d == 1 else NEXT_LAST[0] if d == nz - 1 else NEXT_FAR[p]
+        after = NEXT[p] if d == 1 else NEXT_LAST[p - 2] if d == nz - 1 else NEXT_FAR[p]
         at(done, z_step, u)
         at(done + after[0], f_step, u)
         at(done + after[1], s_step, u)
-        at(done + after[1] + (2.0 if done < 90.0 else 1.0), c_step, u)
+        at(done + after[1] + AFTER, c_step, u)
     queue.sort(key=lambda entry: entry[1])
     previous_time = 0.0
     for n in range(begun, len(queue)):
@@ -671,11 +675,11 @@
 
     def ts_copy(d):
         slot = tsums.at[t]
-        return remote(slot, slot, ts_send.at[d - 1], ts_recv.at[d - 1], (z, lax.rem(t + d, nt)))
-
-    def ts_arrival(d):
-        slot = tsums.at[lax.rem(t + nt - d, nt)]
-        return remote(slot, slot, ts_send.at[d - 1], ts_recv.at[d - 1], partner)
+        return remote(slot, slot, ts_send.at[0], ts_recv.at[0], (z, lax.rem(t + d, nt)))
+
+    def ts_all():
+        slot = tsums.at[pl.ds(0, nt - 1)]
+        return remote(slot, slot, ts_send.at[0], ts_recv.at[0], partner)
 
     for d in range(1, nt):
         ts_copy(d).start()
@@ -683,12 +687,12 @@
     def m_copy(dq):
         slot = maps.at[chip]
         return remote(
-            slot, slot, m_send.at[dq - 1], m_recv.at[dq - 1], (z, 2 * cmod(chip + dq) + core)
+            slot, slot, m_send.at[0], m_recv.at[0], (z, 2 * cmod(chip + dq) + core)
         )
 
-    def m_arrival(dq):
-        slot = maps.at[cmod(chip - dq)]
-        return remote(slot, slot, m_send.at[dq - 1], m_recv.at[dq - 1], partner)
+    def m_all():
+        slot = maps.at[pl.ds(0, nc - 1)]
+        return remote(slot, slot, m_send.at[0], m_recv.at[0], partner)
 
     pm_copy().wait()
     is_second = core == 1
@@ -711,7 +715,7 @@
             whole_done(p)
             if nz > 4:
                 whole_pair(p)("wait_send")
-        for i in range(chunks):
+        for i in range(len(cuts)):
             if nz > 4:
                 @pl.when(outward)
                 def _():
@@ -722,10 +726,10 @@
 
             @pl.when(beside_end)
             def _():
-                sum_copy(i).wait_send()
-
-    for d in range(1, nt):
-        ts_arrival(d).wait_recv()
+                for h in range(2):
+                    sum_copy(i, h).wait_send()
+
+    ts_all().wait_recv()
     plane = tsums[0]
     for k in range(1, nt):
         plane = plane + tsums[k]
@@ -733,34 +737,29 @@
 
     def zs_copy(d):
         slot = zsums.at[z]
-        return remote(slot, slot, zs_send.at[d - 1], zs_recv.at[d - 1], (zmod(z + d), t))
-
-    def zs_arrival(d):
-        slot = zsums.at[zmod(z - d)]
-        return remote(slot, slot, zs_send.at[d - 1], zs_recv.at[d - 1], partner)
+        return remote(slot, slot, zs_send.at[0], zs_recv.at[0], (zmod(z + d), t))
+
+    def zs_all():
+        slot = zsums.at[pl.ds(0, nz - 1)]
+        return remote(slot, slot, zs_send.at[0], zs_recv.at[0], partner)
 
     for d in range(1, nz):
         zs_copy(d).start()
 
-    for dq in range(1, nc):
-        m_arrival(dq).wait_recv()
+    m_all().wait_recv()
     entry = init[...]
     for q in range(nc):
         entry = jnp.where(q < chip, maps[q, 0] * entry + maps[q, 1], entry)
     entry_out[...] = jnp.where(is_second, p_other * entry + s_other, entry)
 
-    for d in range(1, nt):
-        ts_copy(d).wait_send()
-    for dq in range(1, nc):
-        m_copy(dq).wait_send()
-    for d in range(1, nz):
-        zs_arrival(d).wait_recv()
+    ts_all().wait_send()
+    m_all().wait_send()
+    zs_all().wait_recv()
     whole = zsums[0]
     for k in range(1, nz):
         whole = whole + zsums[k]
     total[...] = whole
-    for d in range(1, nz):
-        zs_copy(d).wait_send()
+    zs_all().wait_send()
 
 
 def finish(entries, state, prod, entry, total, states, norm, held, out_sem):
@@ -792,7 +791,7 @@
     parts = 8
     tile = min(256, width)
     units = len(units_of(nz))
-    pieces = 3 if nz == 4 else 4
+    pieces = 2 if nz == 4 else 4
     ways = 1 if nz == 4 else 2
     entries = trajectory.size * nz * nt
     dma = pltpu.SemaphoreType.DMA
@@ -839,16 +838,16 @@
             dma((units,)),
             dma((ways, nz // 2 if ways == 1 else nz, chunks)),
             dma((nz, chunks)),
-            dma((chunks,)),
-            dma((chunks,)),
+            dma((2 * chunks,)),
+            dma((2 * chunks,)),
             dma((2,)),
             dma((2,)),
-            dma((nc - 1,)),
-            dma((nc - 1,)),
-            dma((nt - 1,)),
-            dma((nt - 1,)),
-            dma((nz - 1,)),
-            dma((nz - 1,)),
+            dma((1,)),
+            dma((1,)),
+            dma((1,)),
+            dma((1,)),
+            dma((1,)),
+            dma((1,)),
         ],
         compiler_params=pltpu.CompilerParams(
             collective_id=0, has_side_effects=True, vmem_limit_bytes=56 * 2**20

time: 119 us -> 119 us (level)
  no operation moved by 1% of the time
where the time goes in v3:
time: 119 us
  Pallas kernels  118 us (99%)
    pallas_call x1, Pallas kernels, local(): pl.pallas_call(functools.partial(kernel, nz, nt, chunks, tile), out_shape...  116 us

profile of v3, /device:TPU:0, one launch (start us, length us, event | category | flops | bytes accessed | tf_op | source)
XLA Modules:
  0.0 119.0 jit_solution(13534254880052613873)
XLA Ops:
  0.6 116.3 %shard_map.77 = (f32[64,8,1024]{2,1,0:T(8,128)S(1)}, f32[64,8,1024]{2,1,0:T(8,128)S(1)}, f32[8,1024]{1,0:T(8,128)S(1)}, f32[8,128]{1,0:T(8,128)S(1)}) custom-call(f32[64,8,1024]{2,1,0:T(8,128)} %traj_in.1, f32[8,1024]{1,0:T(8,128)} %init.1, bf16[64,8,1024]{2,1,0:T(8,128)(2,1)} %drive_g_in.1, bf16[64,8,1024]{2,1,0:T(8,128)(2,1)} %drive_c_in.1, ...), custom_call_target="tpu_custom_call" | custom-call | tf_op jit(solution)/shard_map/pallas_call | solution.py:801
  116.9 1.9 %shard_map.78 = (f32[64,8,1024]{2,1,0:T(8,128)}, f32[1,1]{1,0:T(1,128)}) custom-call(f32[64,8,1024]{2,1,0:T(8,128)S(1)} %get-tuple-element.8.state, f32[64,8,1024]{2,1,0:T(8,128)S(1)} %get-tuple-element.9.prod, f32[8,1024]{1,0:T(8,128)S(1)} %get-tuple-element.10.entry, f32[8,128]{1,0:T(8,128)S(1)} %get-tuple-element.11.total), custom_call_target="tpu_custom_call" | custom-call | tf_op jit(solution)/shard_map/pallas_call | solution.py:859
